TPU v7x, 32 devices: a whole 2x2x4 slice. The times are simulated.
32 devices in a mesh: groups: 2 (over x), expert: 16 (over z, y, core).
Axes of the slice: x: 2, y: 2, z: 4, core: 2. Of those that a mesh axis runs over, the one named last changes fastest.
Arguments:
- queries: bfloat16 [256, 4096], P(('groups', 'expert')), parts along dimension 0, may hold values from -150 to 150
- key_cache: bfloat16 [256, 64, 512], P(('groups', 'expert')), parts along dimension 0, may hold values from -7 to 7
- value_cache: bfloat16 [256, 64, 512], P(('groups', 'expert')), parts along dimension 0, may hold values from -6 to 6
- new_key: bfloat16 [256, 512], P(('groups', 'expert')), parts along dimension 0, may hold values from -6 to 6
- new_value: bfloat16 [256, 512], P(('groups', 'expert')), parts along dimension 0, may hold values from -6 to 6
- cache_lengths: int32 [256], P(('groups', 'expert')), parts along dimension 0, may hold values from 2 to 64, as said below
- hidden_in: bfloat16 [2048, 2048], P(('groups', 'expert')), parts along dimension 0, may hold values from -6 to 6
- norm_gain: bfloat16 [2048], replicated, may hold values from 0.5 to 1.5
- router_weight: bfloat16 [2048, 16], replicated, may hold values from -0.125 to 0.125
- expert_ids: int32 [2048, 8], P(('groups', 'expert')), parts along dimension 0, may hold values from 0 to 15, all different within a row; in each aligned block of 64 rows (0 to 63, 64 to 127, ...) at most 64 rows name the same one
- gate_train: bfloat16 [16, 2048, 768], P(None, 'expert'), may hold values from -0.125 to 0.125
- up_train: bfloat16 [16, 2048, 768], P(None, 'expert'), may hold values from -0.125 to 0.125
- down_train: bfloat16 [16, 768, 2048], P(None, 'expert'), may hold values from -0.21875 to 0.21875
Outputs:
- attended: bfloat16 [256, 4096], P(('groups', 'expert')), parts along dimension 0
- expert_mix: bfloat16 [2048, 2048], P(('groups', 'expert')), parts along dimension 0
There are 2 independent parts, one for each index of `groups`. A program takes and returns all parts, laid end to end along the dimension named above; an argument that names none is the same for every part. Nothing has to cross between parts.
Inputs may be any that keep to these rules, and one draw needn't show every extreme that they name: `expert_ids`: each row names 8 different experts; within the rows of one device no expert is named more than 64 times. `cache_lengths`: the first sequence of each device's 8 has all 64 positions filled.
All inputs are finite; a program needn't handle non-finite values.
Results may differ from a plain program's by a relative error of at most 0.0074.
Values may be sent and summed in bfloat16 or wider, within the bound.
No kernel may reach another device: no remote copies, remote signals or barrier semaphores. Data moves between devices by JAX's collectives and lax.ppermute only.
A program may use at most 128 MiB of HBM per device.

v0:
```python
import math

import jax
import jax.numpy as jnp
from jax import lax
from jax.sharding import PartitionSpec as P

HEADS = 32
KV_HEADS = 4
HEAD_DIM = 128
CTX = 64


EPSILON = 1e-06


def rms_normed(hidden_in, norm_gain):
    values = hidden_in.astype(jnp.float32)
    mean_square = jnp.mean(values * values, axis=-1, keepdims=True)
    return (values * lax.rsqrt(mean_square + EPSILON) * norm_gain.astype(jnp.float32)).astype(
        jnp.bfloat16
    )


def attend(queries, key_cache, value_cache, new_key, new_value, cache_lengths):
    seq_count = queries.shape[0]
    group_size = HEADS // KV_HEADS
    query_blocks = queries.reshape(seq_count, KV_HEADS, group_size, HEAD_DIM)
    cached_keys = key_cache.reshape(seq_count, CTX, KV_HEADS, HEAD_DIM)
    cached_values = value_cache.reshape(seq_count, CTX, KV_HEADS, HEAD_DIM)
    fresh_keys = new_key.reshape(seq_count, KV_HEADS, HEAD_DIM)
    fresh_values = new_value.astype(jnp.float32).reshape(seq_count, KV_HEADS, HEAD_DIM)
    score_scale = 1.0 / math.sqrt(HEAD_DIM)
    scores = (
        jnp.einsum("sgrd,scgd->sgrc", query_blocks, cached_keys, preferred_element_type=jnp.float32)
        * score_scale
    )
    own_score = (
        jnp.einsum("sgrd,sgd->sgr", query_blocks, fresh_keys, preferred_element_type=jnp.float32)
        * score_scale
    )
    positions = jnp.arange(CTX, dtype=jnp.int32)
    visible = positions[None, :] < cache_lengths[:, None]
    scores = jnp.where(visible[:, None, None, :], scores, -1e30)
    largest = jnp.maximum(jnp.max(scores, axis=-1), own_score)
    cached_exp = jnp.exp(scores - largest[..., None])
    own_exp = jnp.exp(own_score - largest)
    prob_total = jnp.sum(cached_exp, axis=-1) + own_exp
    cached_prob = (cached_exp / prob_total[..., None]).astype(jnp.bfloat16)
    own_prob = (own_exp / prob_total).astype(jnp.bfloat16).astype(jnp.float32)
    context = jnp.einsum(
        "sgrc,scgd->sgrd", cached_prob, cached_values, preferred_element_type=jnp.float32
    )
    context = context + own_prob[..., None] * fresh_values[:, :, None, :]
    return context.reshape(seq_count, HEADS * HEAD_DIM).astype(jnp.bfloat16)


def expert_rows(received, gate_weight, up_weight, down_weight):
    token_rows = received.reshape(-1, received.shape[2])
    gate_proj = jnp.dot(token_rows, gate_weight, preferred_element_type=jnp.float32)
    up_proj = jnp.dot(token_rows, up_weight, preferred_element_type=jnp.float32)
    hidden_units = (jax.nn.silu(gate_proj) * up_proj).astype(jnp.bfloat16)
    expert_out = jnp.dot(hidden_units, down_weight, preferred_element_type=jnp.float32).astype(
        jnp.bfloat16
    )
    return lax.all_to_all(
        expert_out.reshape(received.shape), "expert", split_axis=0, concat_axis=0, tiled=True
    )


def local(
    queries,
    key_cache,
    value_cache,
    new_key,
    new_value,
    cache_lengths,
    hidden_in,
    norm_gain,
    router_weight,
    expert_ids,
    gate_train,
    up_train,
    down_train,
):
    gate_moved, up_moved, down_moved = (
        lax.all_to_all(gate_train, "expert", split_axis=0, concat_axis=1, tiled=True),
        lax.all_to_all(up_train, "expert", split_axis=0, concat_axis=1, tiled=True),
        lax.all_to_all(down_train, "expert", split_axis=0, concat_axis=1, tiled=True),
    )
    attended = attend(queries, key_cache, value_cache, new_key, new_value, cache_lengths)
    tok_count = hidden_in.shape[0]
    expert_count = router_weight.shape[1]
    top_count = expert_ids.shape[1]
    width = hidden_in.shape[1]
    slot_count = 2 * tok_count * top_count // expert_count
    normed = rms_normed(hidden_in, norm_gain)
    logits = jnp.dot(normed, router_weight, preferred_element_type=jnp.float32)
    expert_range = jnp.arange(expert_count, dtype=jnp.int32)
    picked = expert_ids[:, :, None] == expert_range[None, None, :]
    chosen = jnp.sum(jnp.where(picked, logits[:, None, :], 0.0), axis=-1)
    mixing = jax.nn.softmax(chosen, axis=-1)
    onehot_int = picked.astype(jnp.int32).reshape(-1, expert_count)
    rank_values = jnp.sum((jnp.cumsum(onehot_int, axis=0) - 1) * onehot_int, axis=-1)
    targets = expert_ids.reshape(-1) * slot_count + rank_values
    slot_range = jnp.arange(expert_count * slot_count, dtype=jnp.int32)
    placing = slot_range[:, None] == targets[None, :]
    all_rows, all_ids = (
        lax.all_gather(normed, "expert", axis=0, tiled=True),
        lax.all_gather(expert_ids, "expert", axis=0, tiled=True),
    )
    device_count = lax.axis_size("expert")
    own_index = lax.axis_index("expert")
    own_hits = (all_ids == own_index).astype(jnp.int32).reshape(device_count, tok_count * top_count)
    own_ranks = jnp.cumsum(own_hits, axis=1) - 1
    own_targets = jnp.where(own_hits > 0, own_ranks, -1)
    token_owner = jnp.arange(tok_count * top_count, dtype=jnp.int32) // top_count
    slot_steps = jnp.arange(slot_count, dtype=jnp.int32)
    matches = own_targets[:, None, :] == slot_steps[None, :, None]
    local_token = jnp.sum(jnp.where(matches, token_owner[None, None, :], 0), axis=-1)
    filled = jnp.any(matches, axis=-1)
    row_index = jnp.arange(device_count, dtype=jnp.int32)[:, None] * tok_count + local_token
    taken = jnp.take(all_rows, row_index.reshape(-1), axis=0).reshape(
        device_count, slot_count, width
    )
    received = jnp.where(filled[..., None], taken, jnp.zeros_like(taken))
    returned = expert_rows(received, gate_moved[0], up_moved[0], down_moved[0])
    flat_back = returned.reshape(expert_count * slot_count, width)
    per_assign = lax.dot_general(
        placing.astype(jnp.bfloat16),
        flat_back,
        (((0,), (0,)), ((), ())),
        preferred_element_type=jnp.float32,
    )
    mixed_out = jnp.sum(
        mixing[:, :, None] * per_assign.reshape(tok_count, top_count, width), axis=1
    ).astype(jnp.bfloat16)
    return (attended, mixed_out)


def solution(mesh):
    placed = (
        P(("groups", "expert"), None),
        P(("groups", "expert"), None, None),
        P(("groups", "expert"), None, None),
        P(("groups", "expert"), None),
        P(("groups", "expert"), None),
        P(("groups", "expert")),
        P(("groups", "expert"), None),
        P(),
        P(),
        P(("groups", "expert"), None),
        P(None, "expert", None),
        P(None, "expert", None),
        P(None, "expert", None),
    )
    return jax.shard_map(
        local,
        mesh=mesh,
        in_specs=placed,
        out_specs=(P(("groups", "expert"), None), P(("groups", "expert"), None)),
        check_vma=False,
    )
```

profile of v0, /device:TPU:13, one launch (start us, length us, event | category | flops | bytes accessed | tf_op | source)
XLA Modules:
  0.0 416.2 jit_solution(14784146556622299426)
XLA Ops:
  7.2 76.5 %all_to_all.32 = bf16[16,128,768]{2,1,0:T(8,128)(2,1)} all-to-all(bf16[16,128,768]{2,1,0:T(8,128)(2,1)} %param.23), channel_id=1, replica_groups=mesh['groups'=2,'expert'=16] {'expert'}, dimensions={0} | all-to-all | bytes 6291456 | tf_op jit(solution)/shard_map/all_to_all | solution.py:87
  83.7 5.2 %all-to-all-start.1 = ((bf16[16,128,768]{2,1,0:T(8,128)(2,1)}), bf16[16,128,768]{2,1,0:T(8,128)(2,1)}, u32[]{:S(2)}, u32[]{:S(2)}) async-start(bf16[16,128,768]{2,1,0:T(8,128)(2,1)} %param.24), calls=%async_computation.1 | async-start | bytes 6291456 | tf_op jit(solution)/shard_map/all_to_all | solution.py:88
  89.0 0.2 fusion.7
  89.2 0.8 fusion.9
  90.0 94.1 %all-to-all-done.1 = bf16[16,128,768]{2,1,0:T(8,128)(2,1)} async-done(((bf16[16,128,768]{2,1,0:T(8,128)(2,1)}), bf16[16,128,768]{2,1,0:T(8,128)(2,1)}, u32[]{:S(2)}, u32[]{:S(2)}) %all-to-all-start.1) | async-done | bytes 3145760 | tf_op jit(solution)/shard_map/all_to_all | solution.py:88
  184.2 4.8 %all-to-all-start.2 = ((bf16[16,48,2048]{2,1,0:T(8,128)(2,1)}), bf16[16,48,2048]{2,1,0:T(8,128)(2,1)}, u32[]{:S(2)}, u32[]{:S(2)}) async-start(bf16[16,48,2048]{2,1,0:T(8,128)(2,1)} %param.25), calls=%async_computation.2 | async-start | bytes 6291456 | tf_op jit(solution)/shard_map/all_to_all | solution.py:89
  189.0 79.5 %all-gather = s32[16,64,8]{1,2,0:T(8,128)S(1)} all-gather(s32[1,64,8]{1,2,0:T(8,128)S(1)} %bitcast.77), channel_id=1, replica_groups=mesh['groups'=2,'expert'=16] {'expert'}, dimensions={0}, use_global_device_ids=true | all-gather | bytes 34816 | tf_op jit(solution)/shard_map/all_gather | solution.py:110
  268.5 0.2 copy.59
  268.7 0.2 copy.60
  268.9 0.1 copy.61
  269.0 1.1 reduce-window.16
  270.1 0.2 slice_reduce_fusion
  270.5 0.1 copy.67
  270.6 0.1 copy.64
  270.7 0.4 select_reduce_fusion
  271.3 0.4 fusion
  271.9 11.6 %gather_fusion = bf16[1024,2048]{1,0:T(8,128)(2,1)} fusion(bf16[1024,2048]{1,0:T(8,128)(2,1)} %all-gather.3.cloned.1.call-done, s32[1024]{0:T(1024)S(1)} %broadcast_clamp_fusion), kind=kCustom, calls=%fused_computation | custom fusion | bytes 8392704 | tf_op jit(solution)/shard_map/jit(_take)/gather | solution.py:123
  283.4 8.3 %fusion.32 = f32[1024,768]{1,0:T(8,128)} fusion(bf16[2048,768]{1,0:T(8,128)(2,1)} %bitcast.70, bf16[1024,2048]{1,0:T(8,128)(2,1)} %gather_fusion, pred[1024]{0:T(1024)(128)(4,1)S(1)} %compare_and_fusion, pred[1024]{0:T(1024)(128)(4,1)S(1)} %broadcast_in_dim.86), kind=kOutput, calls=%fused_computation.76 | convolution fusion | flops 3225419776 | bytes 10487808 | tf_op jit(solution)/shard_map/dot_general | solution.py:60
  291.7 13.6 %convolution_convert_fusion = bf16[1024,2048]{1,0:T(8,128)(2,1)} fusion(bf16[768,2048]{1,0:T(8,128)(2,1)} %bitcast.15, f32[1024,768]{1,0:T(8,128)} %fusion.32, bf16[2048,768]{1,0:T(8,128)(2,1)} %bitcast.14, bf16[1024,2048]{1,0:T(8,128)(2,1)} %gather_fusion, pred[1024]{0:T(1024)(128)(4,1)S(1)} %compare_and_fusion, pred[1024]{0:T(1024)(128)(4,1)S(1)} %broadcast_in_dim.86), kind=kOutput, calls=%fused_computation.3 | convolution fusion | flops 6453460992 | bytes 17827840 | tf_op jit(solution)/shard_map/dot_general | solution.py:63
  305.3 5.1 %all-to-all-start.3 = ((bf16[16,64,2048]{2,1,0:T(8,128)(2,1)}), bf16[16,64,2048]{2,1,0:T(8,128)(2,1)}, u32[]{:S(2)}, u32[]{:S(2)}) async-start(bf16[16,64,2048]{2,1,0:T(8,128)(2,1)} %bitcast.69), calls=%async_computation.3 | async-start | bytes 8388608 | tf_op jit(solution)/shard_map/all_to_all | solution.py:66
  310.5 0.1 reshape.285
  310.8 1.2 reduce-window.14
  311.9 0.2 slice_reduce_fusion.1
  312.3 0.2 fusion.17
  312.4 0.5 fusion.33
  312.9 0.2 fusion.14
  313.2 0.3 fusion.5
  313.5 0.7 copy.93
  314.2 0.2 fusion.34
  314.5 0.1 fusion.21
  314.6 88.7 %all-to-all-done.3 = bf16[16,64,2048]{2,1,0:T(8,128)(2,1)} async-done(((bf16[16,64,2048]{2,1,0:T(8,128)(2,1)}), bf16[16,64,2048]{2,1,0:T(8,128)(2,1)}, u32[]{:S(2)}, u32[]{:S(2)}) %all-to-all-start.3) | async-done | bytes 4194336 | tf_op jit(solution)/shard_map/all_to_all | solution.py:66
  403.4 6.0 %multiply_reduce_fusion = bf16[64,2048]{1,0:T(8,128)(2,1)} fusion(bf16[1024,2048,1]{1,0,2:T(8,128)(2,1)} %bitcast.18, f32[64,8]{1,0:T(8,128)S(1)} %copy.55, s32[512]{0:T(512)S(1)} %multiply_add_fusion), kind=kOutput, calls=%fused_computation.1 | convolution fusion | flops 2149974016 | bytes 4460544 | tf_op jit(solution)/shard_map/dot_general | solution.py:129
  (58 shorter events, 1.2 us)
Async XLA Ops:
  7.2 306.0 %copy-start = (bf16[8,64,512]{2,1,0:T(8,128)(2,1)S(1)}, bf16[8,64,512]{2,1,0:T(8,128)(2,1)}, u32[]{:S(2)}) copy-start(bf16[8,64,512]{2,1,0:T(8,128)(2,1)} %param.15) | copy-start | bytes 1572868
  83.7 5.3 %copy-start.8 = (bf16[2048]{0:T(1024)(128)(2,1)S(1)}, bf16[2048]{0:T(1024)(128)(2,1)}, u32[]{:S(2)}) copy-start(bf16[2048]{0:T(1024)(128)(2,1)} %param.20) | copy-start | bytes 12292
  83.7 5.3 %copy-start.2 = (bf16[64,2048]{1,0:T(8,128)(2,1)S(1)}, bf16[64,2048]{1,0:T(8,128)(2,1)}, u32[]{:S(2)}) copy-start(bf16[64,2048]{1,0:T(8,128)(2,1)} %param.19) | copy-start | bytes 786436
  83.7 100.5 %all-to-all-start.1 = ((bf16[16,128,768]{2,1,0:T(8,128)(2,1)}), bf16[16,128,768]{2,1,0:T(8,128)(2,1)}, u32[]{:S(2)}, u32[]{:S(2)}) async-start(bf16[16,128,768]{2,1,0:T(8,128)(2,1)} %param.24), calls=%async_computation.1 | async-start | bytes 6291456 | tf_op jit(solution)/shard_map/all_to_all | solution.py:88
  88.9 182.9 %all-gather.3.cloned.1.call-start = ((), (), s32[]{:S(2)}) async-start(), calls=%async_computation.4 | async-start | bytes 4456448 | tf_op jit(solution)/shard_map/all_gather | solution.py:109
  90.0 99.0 %copy-start.6 = (s32[64,8]{0,1:T(8,128)S(1)}, s32[64,8]{0,1:T(8,128)}, u32[]{:S(2)}) copy-start(s32[64,8]{0,1:T(8,128)} %param.22) | copy-start | bytes 6148
  184.2 107.5 %all-to-all-start.2 = ((bf16[16,48,2048]{2,1,0:T(8,128)(2,1)}), bf16[16,48,2048]{2,1,0:T(8,128)(2,1)}, u32[]{:S(2)}, u32[]{:S(2)}) async-start(bf16[16,48,2048]{2,1,0:T(8,128)(2,1)} %param.25), calls=%async_computation.2 | async-start | bytes 6291456 | tf_op jit(solution)/shard_map/all_to_all | solution.py:89
  305.3 5.4 %copy-start.7 = (bf16[8,512]{1,0:T(8,128)(2,1)S(1)}, bf16[8,512]{1,0:T(8,128)(2,1)}, u32[]{:S(2)}) copy-start(bf16[8,512]{1,0:T(8,128)(2,1)} %param.17) | copy-start | bytes 24580
  305.3 6.9 %copy-start.10 = (s32[8]{0:T(128)S(1)}, s32[8]{0:T(128)}, u32[]{:S(2)}) copy-start(s32[8]{0:T(128)} %param.18) | copy-start | bytes 100
  305.3 7.0 %copy-start.4 = (bf16[8,4096]{1,0:T(8,128)(2,1)S(1)}, bf16[8,4096]{1,0:T(8,128)(2,1)}, u32[]{:S(2)}) copy-start(bf16[8,4096]{1,0:T(8,128)(2,1)} %param.13) | copy-start | bytes 196612
  305.3 7.0 %copy-start.9 = (bf16[8,512]{1,0:T(8,128)(2,1)S(1)}, bf16[8,512]{1,0:T(8,128)(2,1)}, u32[]{:S(2)}) copy-start(bf16[8,512]{1,0:T(8,128)(2,1)} %param.16) | copy-start | bytes 24580
  305.3 7.1 %copy-start.3 = (bf16[8,64,512]{2,1,0:T(8,128)(2,1)S(1)}, bf16[8,64,512]{2,1,0:T(8,128)(2,1)}, u32[]{:S(2)}) copy-start(bf16[8,64,512]{2,1,0:T(8,128)(2,1)} %param.14) | copy-start | bytes 1572868
  305.3 98.1 %all-to-all-start.3 = ((bf16[16,64,2048]{2,1,0:T(8,128)(2,1)}), bf16[16,64,2048]{2,1,0:T(8,128)(2,1)}, u32[]{:S(2)}, u32[]{:S(2)}) async-start(bf16[16,64,2048]{2,1,0:T(8,128)(2,1)} %bitcast.69), calls=%async_computation.3 | async-start | bytes 8388608 | tf_op jit(solution)/shard_map/all_to_all | solution.py:66
  310.4 3.7 copy-start.1
  310.4 3.7 copy-start.5
Sparse Core Ops, SparseCore 0:
  92.5 77.4 all-gather.2
where the time goes:
time: 417 us; the launch traced here: 416 us
  waiting for transfers between devices  183 us (44%)
  blocking collectives  156 us (37%)
  matrix products  28.9 us (7%)
  starting transfers between devices  15.2 us (4%)
  between operations  14.3 us (3%)
  local copies, waits for them, and re-layouts  14 us (3%)
  other arithmetic  4.86 us (1%)
    all_to_all x1, waiting for transfers between devices, local(): lax.all_to_all(up_train, 'expert', split_axis=0, concat_axis=1, tiled=True)  94.1 us
    all_to_all x1, waiting for transfers between devices, expert_rows(): lax.all_to_all(expert_out.reshape(received.shape), 'expert', split_axis=0...  88.7 us
    all_gather x1, blocking collectives, local(): lax.all_gather(expert_ids, 'expert', axis=0, tiled=True)  79.5 us
    all_to_all x1, blocking collectives, local(): lax.all_to_all(gate_train, 'expert', split_axis=0, concat_axis=1, tiled=T...  76.5 us
    dot_general x1, matrix products, expert_rows(): jnp.dot(hidden_units, down_weight, preferred_element_type=jnp.float32)  13.6 us
    gather x1, local copies, waits for them, and re-layouts, local(): jnp.take(all_rows, row_index.reshape(-1), axis=0)  11.6 us
  transfers between devices with their start and end apart: 4, of which 2 were waited for; matrix products, arithmetic and copies ran while one was open for 7% of the time, Pallas kernels for 0%

commit v1 on v0

v1 whole, which is shorter than its diff:
```python
import math

import jax
import jax.numpy as jnp
from jax import lax
from jax.sharding import PartitionSpec as P


HEADS = 32
KV_HEADS = 4
HEAD_DIM = 128
CTX = 64


EPSILON = 1e-06
PIECES = 2


def rms_normed(hidden_in, norm_gain):
    values = hidden_in.astype(jnp.float32)
    mean_square = jnp.mean(values * values, axis=-1, keepdims=True)
    return (values * lax.rsqrt(mean_square + EPSILON) * norm_gain.astype(jnp.float32)).astype(
        jnp.bfloat16
    )


def attend(queries, key_cache, value_cache, new_key, new_value, cache_lengths):
    seq_count = queries.shape[0]
    group_size = HEADS // KV_HEADS
    query_blocks = queries.reshape(seq_count, KV_HEADS, group_size, HEAD_DIM)
    cached_keys = key_cache.reshape(seq_count, CTX, KV_HEADS, HEAD_DIM)
    cached_values = value_cache.reshape(seq_count, CTX, KV_HEADS, HEAD_DIM)
    fresh_keys = new_key.reshape(seq_count, KV_HEADS, HEAD_DIM)
    fresh_values = new_value.astype(jnp.float32).reshape(seq_count, KV_HEADS, HEAD_DIM)
    score_scale = 1.0 / math.sqrt(HEAD_DIM)
    scores = (
        jnp.einsum("sgrd,scgd->sgrc", query_blocks, cached_keys, preferred_element_type=jnp.float32)
        * score_scale
    )
    own_score = (
        jnp.einsum("sgrd,sgd->sgr", query_blocks, fresh_keys, preferred_element_type=jnp.float32)
        * score_scale
    )
    positions = jnp.arange(CTX, dtype=jnp.int32)
    visible = positions[None, :] < cache_lengths[:, None]
    scores = jnp.where(visible[:, None, None, :], scores, -1e30)
    largest = jnp.maximum(jnp.max(scores, axis=-1), own_score)
    cached_exp = jnp.exp(scores - largest[..., None])
    own_exp = jnp.exp(own_score - largest)
    prob_total = jnp.sum(cached_exp, axis=-1) + own_exp
    cached_prob = (cached_exp / prob_total[..., None]).astype(jnp.bfloat16)
    own_prob = (own_exp / prob_total).astype(jnp.bfloat16).astype(jnp.float32)
    context = jnp.einsum(
        "sgrc,scgd->sgrd", cached_prob, cached_values, preferred_element_type=jnp.float32
    )
    context = context + own_prob[..., None] * fresh_values[:, :, None, :]
    return context.reshape(seq_count, HEADS * HEAD_DIM).astype(jnp.bfloat16)


def shifted(value, step):
    count = lax.axis_size("groups")
    return lax.ppermute(value, "groups", [(i, (i + step) % count) for i in range(count)])


def moved(train, part, parts, piece=0, pieces=1):
    width = train.shape[2] // (parts * pieces)
    own = lax.dynamic_slice_in_dim(train, (part * pieces + piece) * width, width, axis=2)
    block = lax.all_to_all(own, "expert", split_axis=0, concat_axis=0, tiled=True)
    return block.reshape(-1, width)


def summed(partial):
    count = lax.axis_size("expert")
    index = lax.axis_index("expert")
    if count & (count - 1):
        return lax.psum_scatter(
            partial.astype(jnp.bfloat16), "expert", scatter_dimension=0, tiled=True
        )
    total_bits = count.bit_length() - 1
    low_bits = min(2, total_bits)
    order = list(range(low_bits)) + list(range(total_bits - 1, low_bits - 1, -1))
    rows, width = partial.shape
    left = sorted(order)
    kept = partial.reshape((2,) * total_bits + (rows // count, width))
    for bit in order:
        axis = len(left) - 1 - left.index(bit)
        side = (index >> bit) & 1
        out = lax.dynamic_index_in_dim(kept, 1 - side, axis, keepdims=False)
        own = lax.dynamic_index_in_dim(kept, side, axis, keepdims=False)
        pairs = [(i, i ^ (1 << bit)) for i in range(count)]
        came = lax.ppermute(out.astype(jnp.bfloat16), "expert", pairs)
        kept = own.astype(jnp.float32) + came.astype(jnp.float32)
        left.remove(bit)
    return kept.astype(jnp.bfloat16)


def local(
    queries,
    key_cache,
    value_cache,
    new_key,
    new_value,
    cache_lengths,
    hidden_in,
    norm_gain,
    router_weight,
    expert_ids,
    gate_train,
    up_train,
    down_train,
):
    parts = lax.axis_size("groups")
    part = lax.axis_index("groups")
    own_index = lax.axis_index("expert")
    tok_count, width = hidden_in.shape
    expert_count = router_weight.shape[1]

    normed = rms_normed(hidden_in, norm_gain)
    logits = jnp.dot(normed, router_weight, preferred_element_type=jnp.float32)
    expert_range = jnp.arange(expert_count, dtype=jnp.int32)
    picked = jnp.any(expert_ids[:, :, None] == expert_range[None, None, :], axis=1)
    largest = jnp.max(jnp.where(picked, logits, -jnp.inf), axis=-1, keepdims=True)
    raised = jnp.where(picked, jnp.exp(jnp.where(picked, logits - largest, 0.0)), 0.0)
    mixing = raised / jnp.sum(raised, axis=-1, keepdims=True)
    high = lax.reduce_precision(mixing, 8, 7)
    low = mixing - high
    spare = -(2 * expert_count) % 128
    sent = jnp.concatenate(
        (
            normed,
            high.astype(jnp.bfloat16),
            low.astype(jnp.bfloat16),
            jnp.zeros((tok_count, spare), jnp.bfloat16),
        ),
        axis=1,
    )
    everything = lax.all_gather(sent, "expert", axis=0, tiled=True)

    gate_own = moved(gate_train, part, parts)
    up_own = moved(up_train, part, parts)
    down_pieces = [moved(down_train, part, parts, i, PIECES) for i in range(PIECES)]

    attended = attend(queries, key_cache, value_cache, new_key, new_value, cache_lengths)

    all_rows = everything[:, :width]
    tail = everything[:, width:].astype(jnp.float32)
    lane = jnp.arange(tail.shape[1], dtype=jnp.int32)
    mine = (lane == own_index) | (lane == own_index + expert_count)
    weight = jnp.sum(jnp.where(mine[None, :], tail, 0.0), axis=1, keepdims=True)

    unit_width = gate_own.shape[1]
    hidden_units = jnp.zeros((all_rows.shape[0], unit_width * parts), jnp.bfloat16)
    for step in range(parts):
        gate_weight = gate_own if step == 0 else shifted(gate_own, step)
        up_weight = up_own if step == 0 else shifted(up_own, step)
        gate_proj = jnp.dot(all_rows, gate_weight, preferred_element_type=jnp.float32)
        up_proj = jnp.dot(all_rows, up_weight, preferred_element_type=jnp.float32)
        units = (jax.nn.silu(gate_proj) * up_proj).astype(jnp.bfloat16)
        place = (part + parts - step) % parts
        hidden_units = lax.dynamic_update_slice_in_dim(
            hidden_units, units, place * unit_width, axis=1
        )

    out_width = down_pieces[0].shape[1]
    mixed_out = jnp.zeros((tok_count, width), jnp.bfloat16)
    for step in range(parts):
        for number, down_own in enumerate(down_pieces):
            down_weight = down_own if step == 0 else shifted(down_own, step)
            expert_out = jnp.dot(hidden_units, down_weight, preferred_element_type=jnp.float32)
            reduced = summed((weight * expert_out).astype(jnp.bfloat16))
            place = ((part + parts - step) % parts) * PIECES + number
            mixed_out = lax.dynamic_update_slice_in_dim(
                mixed_out, reduced, place * out_width, axis=1
            )
    return (attended, mixed_out)


def solution(mesh):
    placed = (
        P(("groups", "expert"), None),
        P(("groups", "expert"), None, None),
        P(("groups", "expert"), None, None),
        P(("groups", "expert"), None),
        P(("groups", "expert"), None),
        P(("groups", "expert")),
        P(("groups", "expert"), None),
        P(),
        P(),
        P(("groups", "expert"), None),
        P(None, "expert", None),
        P(None, "expert", None),
        P(None, "expert", None),
    )

    return jax.shard_map(
        local,
        mesh=mesh,
        in_specs=placed,
        out_specs=(P(("groups", "expert"), None), P(("groups", "expert"), None)),
        check_vma=False,
    )
```

time: 417 us -> 301 us (0.72)
  blocking collectives: 156 us -> 0 us
  starting transfers between devices: 15.2 us -> 42.1 us
  waiting for transfers between devices: 183 us -> 199 us
    all_gather x1 -> x0, blocking collectives: 79.5 us -> none  [local(): lax.all_gather(expert_ids, 'expert', axis=0, tiled=True)]
    all_to_all x1 -> x0, blocking collectives: 76.5 us -> none  [local(): lax.all_to_all(gate_train, 'expert', split_axis=0, concat_axis=1, tiled=T...]
    ppermute x0 -> x20, waiting for transfers between devices: none -> 74.5 us  [the longest x4 54.2 us: shifted(): lax.ppermute(value, 'groups', [(i, (i + step) % count) for i in range(cou...]
    all_to_all x3 -> x4, waiting for transfers between devices: 183 us -> 124 us  [moved(): lax.all_to_all(own, 'expert', split_axis=0, concat_axis=0, tiled=True)]
    ppermute x0 -> x20, starting transfers between devices: none -> 21 us  [the longest x16 17 us: summed(): came = lax.ppermute(out.astype(jnp.bfloat16), 'expert', pairs)]
    gather x1 -> x0, local copies, waits for them, and re-layouts: 11.6 us -> none  [local(): jnp.take(all_rows, row_index.reshape(-1), axis=0)]
    dynamic_slice x0 -> x9, local copies, waits for them, and re-layouts: none -> 7.5 us  [the longest x3 6.92 us: moved(): lax.dynamic_slice_in_dim(train, (part * pieces + piece) * width, width, a...]
    all_to_all x3 -> x4, starting transfers between devices: 15.2 us -> 21.1 us  [moved(): lax.all_to_all(own, 'expert', split_axis=0, concat_axis=0, tiled=True)]
  transfers between devices with their start and end apart: 4 -> 25, of which waited for: 2 -> 12; matrix products, arithmetic and copies ran while one was open for 7% -> 12% of each run, Pallas kernels for 0% -> 0%
where the time goes in v1:
time: 301 us; the launch traced here: 297 us
  waiting for transfers between devices  199 us (66%)
  starting transfers between devices  42.1 us (14%)
  matrix products  28.4 us (9%)
  between operations  14.5 us (5%)
  local copies, waits for them, and re-layouts  10.4 us (3%)
    all_to_all x4, waiting for transfers between devices, moved(): lax.all_to_all(own, 'expert', split_axis=0, concat_axis=0, tiled=True)  124 us
    ppermute x4, waiting for transfers between devices, shifted(): lax.ppermute(value, 'groups', [(i, (i + step) % count) for i in range(cou...  54.2 us
    all_to_all x4, starting transfers between devices, moved(): lax.all_to_all(own, 'expert', split_axis=0, concat_axis=0, tiled=True)  21.1 us
    ppermute x16, waiting for transfers between devices, summed(): came = lax.ppermute(out.astype(jnp.bfloat16), 'expert', pairs)  20.3 us
    ppermute x16, starting transfers between devices, summed(): came = lax.ppermute(out.astype(jnp.bfloat16), 'expert', pairs)  17 us
    dot_general x2, matrix products, local(): jnp.dot(all_rows, gate_weight, preferred_element_type=jnp.float32)  8.87 us
    dot_general x4, matrix products, local(): jnp.dot(hidden_units, down_weight, preferred_element_type=jnp.float32)  8.41 us
    dot_general x2, matrix products, local(): up_proj = jnp.dot(all_rows, up_weight, preferred_element_type=jnp.float32)  7.91 us
  transfers between devices with their start and end apart: 25, of which 12 were waited for; matrix products, arithmetic and copies ran while one was open for 12% of the time, Pallas kernels for 0%

profile of v1, /device:TPU:13, one launch (start us, length us, event | category | flops | bytes accessed | tf_op | source)
XLA Modules:
  0.0 297.0 jit_solution(5100852528142248874)
XLA Ops:
  7.2 2.8 constant_dynamic-slice_fusion.6
  10.0 6.7 %all-to-all-start.2 = ((bf16[16,48,512]{2,1,0:T(8,128)(2,1)}), bf16[16,48,512]{2,1,0:T(8,128)(2,1)}, u32[]{:S(2)}, u32[]{:S(2)}) async-start(bf16[16,48,512]{2,1,0:T(8,128)(2,1)} %get-tuple-element.3), calls=%async_computation.2 | async-start | bytes 1572864 | tf_op jit(solution)/shard_map/all_to_all | solution.py:68
  19.4 25.6 %all-to-all-done.2 = bf16[16,48,512]{2,1,0:T(8,128)(2,1)} async-done(((bf16[16,48,512]{2,1,0:T(8,128)(2,1)}), bf16[16,48,512]{2,1,0:T(8,128)(2,1)}, u32[]{:S(2)}, u32[]{:S(2)}) %all-to-all-start.2) | async-done | bytes 786464 | tf_op jit(solution)/shard_map/all_to_all | solution.py:68
  45.0 4.8 %all-to-all-start.3 = ((bf16[16,48,512]{2,1,0:T(8,128)(2,1)}), bf16[16,48,512]{2,1,0:T(8,128)(2,1)}, u32[]{:S(2)}, u32[]{:S(2)}) async-start(bf16[16,48,512]{2,1,0:T(8,128)(2,1)} %get-tuple-element.2), calls=%async_computation.3 | async-start | bytes 1572864 | tf_op jit(solution)/shard_map/all_to_all | solution.py:68
  51.1 35.3 %all-to-all-done.3 = bf16[16,48,512]{2,1,0:T(8,128)(2,1)} async-done(((bf16[16,48,512]{2,1,0:T(8,128)(2,1)}), bf16[16,48,512]{2,1,0:T(8,128)(2,1)}, u32[]{:S(2)}, u32[]{:S(2)}) %all-to-all-start.3) | async-done | bytes 786464 | tf_op jit(solution)/shard_map/all_to_all | solution.py:68
  86.4 4.8 %all-to-all-start = ((bf16[16,128,384]{2,1,0:T(8,128)(2,1)}), bf16[16,128,384]{2,1,0:T(8,128)(2,1)}, u32[]{:S(2)}, u32[]{:S(2)}) async-start(bf16[16,128,384]{2,1,0:T(8,128)(2,1)} %constant_dynamic-slice_fusion.11), calls=%async_computation | async-start | bytes 3145728 | tf_op jit(solution)/shard_map/all_to_all | solution.py:68
  91.3 2.8 constant_dynamic-slice_fusion.10
  94.0 33.5 %all-to-all-done = bf16[16,128,384]{2,1,0:T(8,128)(2,1)} async-done(((bf16[16,128,384]{2,1,0:T(8,128)(2,1)}), bf16[16,128,384]{2,1,0:T(8,128)(2,1)}, u32[]{:S(2)}, u32[]{:S(2)}) %all-to-all-start) | async-done | bytes 1572896 | tf_op jit(solution)/shard_map/all_to_all | solution.py:68
  127.5 4.8 %all-to-all-start.1 = ((bf16[16,128,384]{2,1,0:T(8,128)(2,1)}), bf16[16,128,384]{2,1,0:T(8,128)(2,1)}, u32[]{:S(2)}, u32[]{:S(2)}) async-start(bf16[16,128,384]{2,1,0:T(8,128)(2,1)} %constant_dynamic-slice_fusion.10), calls=%async_computation.1 | async-start | bytes 3145728 | tf_op jit(solution)/shard_map/all_to_all | solution.py:68
  132.6 1.5 fusion.57
  135.6 1.4 fusion.15
  139.1 29.8 %all-to-all-done.1 = bf16[16,128,384]{2,1,0:T(8,128)(2,1)} async-done(((bf16[16,128,384]{2,1,0:T(8,128)(2,1)}), bf16[16,128,384]{2,1,0:T(8,128)(2,1)}, u32[]{:S(2)}, u32[]{:S(2)}) %all-to-all-start.1) | async-done | bytes 1572896 | tf_op jit(solution)/shard_map/all_to_all | solution.py:68
  170.1 5.1 %fusion.6 = f32[1024,384]{1,0:T(8,128)S(1)} fusion(bf16[2048,384]{1,0:T(8,128)(2,1)} %bitcast.6, bf16[1024,2176]{1,0:T(8,128)(2,1)} %all-gather.2.cloned.1.call-done), kind=kOutput, calls=%fused_computation.6 | convolution fusion | flops 1610612736 | bytes 7340032 | tf_op jit(solution)/shard_map/dot_general | solution.py:156
  175.3 3.7 %fusion.2 = f32[1024,384]{1,0:T(8,128)S(1)} fusion(bf16[2048,384]{1,0:T(8,128)(2,1)} %collective-permute-done, bf16[1024,2176]{1,0:T(8,128)(2,1)S(1)} %copy-done.5), kind=kOutput, calls=%fused_computation.2 | convolution fusion | flops 1610612736 | bytes 7340032 | tf_op jit(solution)/shard_map/dot_general | solution.py:156
  179.1 4.0 %fusion.10 = bf16[1024,768]{1,0:T(8,128)(2,1)S(1)} fusion(bf16[1024,768]{1,0:T(8,128)(2,1)S(1)} %broadcast_in_dim.63, s32[]{:T(128)S(6)} %select_n.124, bf16[2048,384]{1,0:T(8,128)(2,1)} %bitcast.7, bf16[1024,2176]{1,0:T(8,128)(2,1)S(1)} %copy-done.5, f32[1024,384]{1,0:T(8,128)S(1)} %fusion.6), kind=kOutput, calls=%fused_computation.14 | convolution fusion | flops 1612972032 | bytes 8126468 | tf_op jit(solution)/shard_map/dot_general | solution.py:157
  183.2 54.1 %collective-permute-done.1 = bf16[2048,384]{1,0:T(8,128)(2,1)} collective-permute-done((bf16[2048,384]{1,0:T(8,128)(2,1)}, bf16[2048,384]{1,0:T(8,128)(2,1)}, u32[]{:S(2)}, u32[]{:S(2)}) %collective-permute-start.1) | collective-permute-done | bytes 1572896 | tf_op jit(solution)/shard_map/ppermute | solution.py:62
  237.4 4.0 %fusion.16 = bf16[1024,768]{1,0:T(8,128)(2,1)S(1)} fusion(bf16[1024,768]{1,0:T(8,128)(2,1)S(1)} %fusion.10, s32[]{:T(128)S(6)} %select_n.126, f32[1024,384]{1,0:T(8,128)S(1)} %fusion.2, bf16[2048,384]{1,0:T(8,128)(2,1)} %collective-permute-done.1, bf16[1024,2176]{1,0:T(8,128)(2,1)S(1)} %copy-done.5), kind=kOutput, calls=%fused_computation.24 | convolution fusion | flops 1612972032 | bytes 8126468 | tf_op jit(solution)/shard_map/dot_general | solution.py:157
  241.4 2.1 multiply_convert_fusion.1
  243.5 2.1 multiply_convert_fusion
  247.2 2.1 multiply_convert_fusion.3
  249.4 2.1 multiply_convert_fusion.2
  256.5 3.6 %collective-permute-done.17 = bf16[2,2,64,512]{3,2,1,0:T(8,128)(2,1)S(1)} collective-permute-done((bf16[2,2,64,512]{3,2,1,0:T(8,128)(2,1)S(1)}, bf16[2,2,64,512]{3,2,1,0:T(8,128)(2,1)S(1)}, u32[]{:S(2)}, u32[]{:S(2)}) %collective-permute-start.17) | collective-permute-done | bytes 262176 | tf_op jit(solution)/shard_map/ppermute | solution.py:91
  260.2 2.1 collective-permute-start.18
  262.4 3.4 %collective-permute-done.12 = bf16[2,2,64,512]{3,2,1,0:T(8,128)(2,1)S(1)} collective-permute-done((bf16[2,2,64,512]{3,2,1,0:T(8,128)(2,1)S(1)}, bf16[2,2,64,512]{3,2,1,0:T(8,128)(2,1)S(1)}, u32[]{:S(2)}, u32[]{:S(2)}) %collective-permute-start.12) | collective-permute-done | bytes 262176 | tf_op jit(solution)/shard_map/ppermute | solution.py:91
  265.8 2.1 collective-permute-start.13
  268.0 3.4 %collective-permute-done.7 = bf16[2,2,64,512]{3,2,1,0:T(8,128)(2,1)S(1)} collective-permute-done((bf16[2,2,64,512]{3,2,1,0:T(8,128)(2,1)S(1)}, bf16[2,2,64,512]{3,2,1,0:T(8,128)(2,1)S(1)}, u32[]{:S(2)}, u32[]{:S(2)}) %collective-permute-start.7) | collective-permute-done | bytes 262176 | tf_op jit(solution)/shard_map/ppermute | solution.py:91
  271.5 2.1 collective-permute-start.8
  273.6 3.4 %collective-permute-done.3 = bf16[2,2,64,512]{3,2,1,0:T(8,128)(2,1)S(1)} collective-permute-done((bf16[2,2,64,512]{3,2,1,0:T(8,128)(2,1)S(1)}, bf16[2,2,64,512]{3,2,1,0:T(8,128)(2,1)S(1)}, u32[]{:S(2)}, u32[]{:S(2)}) %collective-permute-start.3) | collective-permute-done | bytes 262176 | tf_op jit(solution)/shard_map/ppermute | solution.py:91
  277.1 2.1 collective-permute-start.4
  281.0 4.0 %collective-permute-done.4 = bf16[2,64,512]{2,1,0:T(8,128)(2,1)S(1)} collective-permute-done((bf16[2,64,512]{2,1,0:T(8,128)(2,1)S(1)}, bf16[2,64,512]{2,1,0:T(8,128)(2,1)S(1)}, u32[]{:S(2)}, u32[]{:S(2)}) %collective-permute-start.4) | collective-permute-done | bytes 131104 | tf_op jit(solution)/shard_map/ppermute | solution.py:91
  285.2 1.5 collective-permute-start.9
  286.7 1.5 collective-permute-done.5
  (112 shorter events, 20.1 us)
Async XLA Ops:
  7.2 42.6 %copy-start = (bf16[16,128,768]{2,1,0:T(8,128)(2,1)S(1)}, bf16[16,128,768]{2,1,0:T(8,128)(2,1)}, u32[]{:S(2)}) copy-start(bf16[16,128,768]{2,1,0:T(8,128)(2,1)} %param.23) | copy-start | bytes 9437188
  10.0 6.8 %copy-start.1 = (bf16[64,2048]{1,0:T(8,128)(2,1)S(1)}, bf16[64,2048]{1,0:T(8,128)(2,1)}, u32[]{:S(2)}) copy-start(bf16[64,2048]{1,0:T(8,128)(2,1)} %param.19) | copy-start | bytes 786436
  10.0 8.0 %copy-start.4 = (bf16[2048,16]{0,1:T(8,128)(2,1)S(1)}, bf16[2048,16]{0,1:T(8,128)(2,1)}, u32[]{:S(2)}) copy-start(bf16[2048,16]{0,1:T(8,128)(2,1)} %param.21) | copy-start | bytes 196612
  10.0 35.0 %all-to-all-start.2 = ((bf16[16,48,512]{2,1,0:T(8,128)(2,1)}), bf16[16,48,512]{2,1,0:T(8,128)(2,1)}, u32[]{:S(2)}, u32[]{:S(2)}) async-start(bf16[16,48,512]{2,1,0:T(8,128)(2,1)} %get-tuple-element.3), calls=%async_computation.2 | async-start | bytes 1572864 | tf_op jit(solution)/shard_map/all_to_all | solution.py:68
  16.7 153.5 %all-gather.2.cloned.1.call-start = ((), (), s32[]{:S(2)}) async-start(), calls=%async_computation.4 | async-start | bytes 4734976 | tf_op jit(solution)/shard_map/all_gather | solution.py:137
  45.0 41.4 %all-to-all-start.3 = ((bf16[16,48,512]{2,1,0:T(8,128)(2,1)}), bf16[16,48,512]{2,1,0:T(8,128)(2,1)}, u32[]{:S(2)}, u32[]{:S(2)}) async-start(bf16[16,48,512]{2,1,0:T(8,128)(2,1)} %get-tuple-element.2), calls=%async_computation.3 | async-start | bytes 1572864 | tf_op jit(solution)/shard_map/all_to_all | solution.py:68
  86.4 41.1 %all-to-all-start = ((bf16[16,128,384]{2,1,0:T(8,128)(2,1)}), bf16[16,128,384]{2,1,0:T(8,128)(2,1)}, u32[]{:S(2)}, u32[]{:S(2)}) async-start(bf16[16,128,384]{2,1,0:T(8,128)(2,1)} %constant_dynamic-slice_fusion.11), calls=%async_computation | async-start | bytes 3145728 | tf_op jit(solution)/shard_map/all_to_all | solution.py:68
  94.0 38.3 %copy-start.10 = (s32[8]{0:T(128)S(1)}, s32[8]{0:T(128)}, u32[]{:S(2)}) copy-start(s32[8]{0:T(128)} %param.18) | copy-start | bytes 100
  94.0 38.4 %copy-start.3 = (bf16[8,4096]{1,0:T(8,128)(2,1)S(1)}, bf16[8,4096]{1,0:T(8,128)(2,1)}, u32[]{:S(2)}) copy-start(bf16[8,4096]{1,0:T(8,128)(2,1)} %param.13) | copy-start | bytes 196612
  94.0 38.4 %copy-start.9 = (bf16[8,512]{1,0:T(8,128)(2,1)S(1)}, bf16[8,512]{1,0:T(8,128)(2,1)}, u32[]{:S(2)}) copy-start(bf16[8,512]{1,0:T(8,128)(2,1)} %param.16) | copy-start | bytes 24580
  94.0 41.3 %copy-start.6 = (bf16[8,512]{1,0:T(8,128)(2,1)S(1)}, bf16[8,512]{1,0:T(8,128)(2,1)}, u32[]{:S(2)}) copy-start(bf16[8,512]{1,0:T(8,128)(2,1)} %param.17) | copy-start | bytes 24580
  127.5 41.4 %all-to-all-start.1 = ((bf16[16,128,384]{2,1,0:T(8,128)(2,1)}), bf16[16,128,384]{2,1,0:T(8,128)(2,1)}, u32[]{:S(2)}, u32[]{:S(2)}) async-start(bf16[16,128,384]{2,1,0:T(8,128)(2,1)} %constant_dynamic-slice_fusion.10), calls=%async_computation.1 | async-start | bytes 3145728 | tf_op jit(solution)/shard_map/all_to_all | solution.py:68
  134.1 41.2 %collective-permute-start = (bf16[2048,384]{1,0:T(8,128)(2,1)}, bf16[2048,384]{1,0:T(8,128)(2,1)}, u32[]{:S(2)}, u32[]{:S(2)}) collective-permute-start(bf16[2048,384]{1,0:T(8,128)(2,1)} %bitcast.6), channel_id=1, source_target_pairs={{0,16},{16,0},{1,17},{17,1},{2,18},{18,2},{3,19},{19,3},{4,20},{20... | collective-permute-start | bytes 4718600 | tf_op jit(solution)/shard_map/ppermute | solution.py:62
  137.6 103.7 %collective-permute-start.10 = (bf16[768,512]{1,0:T(8,128)(2,1)}, bf16[768,512]{1,0:T(8,128)(2,1)}, u32[]{:S(2)}, u32[]{:S(2)}) collective-permute-start(bf16[768,512]{1,0:T(8,128)(2,1)} %bitcast.8), channel_id=1, source_target_pairs={{0,16},{16,0},{1,17},{17,1},{2,18},{18,2},{3,19},{19,3},{4,20},{20... | collective-permute-start | bytes 2359304 | tf_op jit(solution)/shard_map/ppermute | solution.py:62
  137.9 105.6 %collective-permute-start.15 = (bf16[768,512]{1,0:T(8,128)(2,1)}, bf16[768,512]{1,0:T(8,128)(2,1)}, u32[]{:S(2)}, u32[]{:S(2)}) collective-permute-start(bf16[768,512]{1,0:T(8,128)(2,1)} %bitcast.18), channel_id=1, source_target_pairs={{0,16},{16,0},{1,17},{17,1},{2,18},{18,2},{3,19},{19,3},{4,20},{20... | collective-permute-start | bytes 2359304 | tf_op jit(solution)/shard_map/ppermute | solution.py:62
  168.9 68.5 %collective-permute-start.1 = (bf16[2048,384]{1,0:T(8,128)(2,1)}, bf16[2048,384]{1,0:T(8,128)(2,1)}, u32[]{:S(2)}, u32[]{:S(2)}) collective-permute-start(bf16[2048,384]{1,0:T(8,128)(2,1)} %bitcast.7), channel_id=1, source_target_pairs={{0,16},{16,0},{1,17},{17,1},{2,18},{18,2},{3,19},{19,3},{4,20},{20... | collective-permute-start | bytes 4718600 | tf_op jit(solution)/shard_map/ppermute | solution.py:62
  245.9 6.6 %collective-permute-start.16 = (bf16[2,2,2,64,512]{4,3,1,0,2:T(8,128)(2,1)S(1)}, bf16[2,2,2,64,512]{4,3,1,0,2:T(8,128)(2,1)S(1)}, u32[]{:S(2)}, u32[]{:S(2)}) collective-permute-start(bf16[2,2,2,64,512]{4,3,1,0,2:T(8,128)(2,1)S(1)} %bitcast.155), channel_id=1, source_target_pairs={{0,1},{1,0},{2,3},{3,2},{4,5},{5,4},{6,7},{7,6},{8,9},{9,8},{10,11... | collective-permute-start | bytes 1572872 | tf_op jit(solution)/shard_map/ppermute | solution.py:91
  249.3 3.7 %collective-permute-start.11 = (bf16[2,2,2,64,512]{4,3,1,0,2:T(8,128)(2,1)S(1)}, bf16[2,2,2,64,512]{4,3,1,0,2:T(8,128)(2,1)S(1)}, u32[]{:S(2)}, u32[]{:S(2)}) collective-permute-start(bf16[2,2,2,64,512]{4,3,1,0,2:T(8,128)(2,1)S(1)} %bitcast.153), channel_id=1, source_target_pairs={{0,1},{1,0},{2,3},{3,2},{4,5},{5,4},{6,7},{7,6},{8,9},{9,8},{10,11... | collective-permute-start | bytes 1572872 | tf_op jit(solution)/shard_map/ppermute | solution.py:91
  251.8 2.7 collective-permute-start.6
  252.4 2.6 collective-permute-start.2
  252.7 7.4 %collective-permute-start.17 = (bf16[2,2,64,512]{3,2,1,0:T(8,128)(2,1)S(1)}, bf16[2,2,64,512]{3,2,1,0:T(8,128)(2,1)S(1)}, u32[]{:S(2)}, u32[]{:S(2)}) collective-permute-start(bf16[2,2,64,512]{3,2,1,0:T(8,128)(2,1)S(1)} %fusion.27), channel_id=1, source_target_pairs={{0,2},{1,3},{2,0},{3,1},{4,6},{5,7},{6,4},{7,5},{8,10},{9,11},{10,... | collective-permute-start | bytes 786440 | tf_op jit(solution)/shard_map/ppermute | solution.py:91
  253.2 12.5 %collective-permute-start.12 = (bf16[2,2,64,512]{3,2,1,0:T(8,128)(2,1)S(1)}, bf16[2,2,64,512]{3,2,1,0:T(8,128)(2,1)S(1)}, u32[]{:S(2)}, u32[]{:S(2)}) collective-permute-start(bf16[2,2,64,512]{3,2,1,0:T(8,128)(2,1)S(1)} %fusion.26), channel_id=1, source_target_pairs={{0,2},{1,3},{2,0},{3,1},{4,6},{5,7},{6,4},{7,5},{8,10},{9,11},{10,... | collective-permute-start | bytes 786440 | tf_op jit(solution)/shard_map/ppermute | solution.py:91
  254.7 16.7 %collective-permute-start.7 = (bf16[2,2,64,512]{3,2,1,0:T(8,128)(2,1)S(1)}, bf16[2,2,64,512]{3,2,1,0:T(8,128)(2,1)S(1)}, u32[]{:S(2)}, u32[]{:S(2)}) collective-permute-start(bf16[2,2,64,512]{3,2,1,0:T(8,128)(2,1)S(1)} %fusion.25), channel_id=1, source_target_pairs={{0,2},{1,3},{2,0},{3,1},{4,6},{5,7},{6,4},{7,5},{8,10},{9,11},{10,... | collective-permute-start | bytes 786440 | tf_op jit(solution)/shard_map/ppermute | solution.py:91
  255.2 21.7 %collective-permute-start.3 = (bf16[2,2,64,512]{3,2,1,0:T(8,128)(2,1)S(1)}, bf16[2,2,64,512]{3,2,1,0:T(8,128)(2,1)S(1)}, u32[]{:S(2)}, u32[]{:S(2)}) collective-permute-start(bf16[2,2,64,512]{3,2,1,0:T(8,128)(2,1)S(1)} %fusion.24), channel_id=1, source_target_pairs={{0,2},{1,3},{2,0},{3,1},{4,6},{5,7},{6,4},{7,5},{8,10},{9,11},{10,... | collective-permute-start | bytes 786440 | tf_op jit(solution)/shard_map/ppermute | solution.py:91
  260.2 19.0 %collective-permute-start.18 = (bf16[2,64,512]{2,1,0:T(8,128)(2,1)S(1)}, bf16[2,64,512]{2,1,0:T(8,128)(2,1)S(1)}, u32[]{:S(2)}, u32[]{:S(2)}) collective-permute-start(bf16[2,64,512]{2,1,0:T(8,128)(2,1)S(1)} %fusion.31), channel_id=1, source_target_pairs={{0,8},{1,9},{2,10},{3,11},{4,12},{5,13},{6,14},{7,15},{8,0},{9,1},... | collective-permute-start | bytes 393224 | tf_op jit(solution)/shard_map/ppermute | solution.py:91
  265.8 13.8 %collective-permute-start.13 = (bf16[2,64,512]{2,1,0:T(8,128)(2,1)S(1)}, bf16[2,64,512]{2,1,0:T(8,128)(2,1)S(1)}, u32[]{:S(2)}, u32[]{:S(2)}) collective-permute-start(bf16[2,64,512]{2,1,0:T(8,128)(2,1)S(1)} %fusion.30), channel_id=1, source_target_pairs={{0,8},{1,9},{2,10},{3,11},{4,12},{5,13},{6,14},{7,15},{8,0},{9,1},... | collective-permute-start | bytes 393224 | tf_op jit(solution)/shard_map/ppermute | solution.py:91
  271.5 13.6 %collective-permute-start.8 = (bf16[2,64,512]{2,1,0:T(8,128)(2,1)S(1)}, bf16[2,64,512]{2,1,0:T(8,128)(2,1)S(1)}, u32[]{:S(2)}, u32[]{:S(2)}) collective-permute-start(bf16[2,64,512]{2,1,0:T(8,128)(2,1)S(1)} %fusion.29), channel_id=1, source_target_pairs={{0,8},{1,9},{2,10},{3,11},{4,12},{5,13},{6,14},{7,15},{8,0},{9,1},... | collective-permute-start | bytes 393224 | tf_op jit(solution)/shard_map/ppermute | solution.py:91
  277.1 7.9 %collective-permute-start.4 = (bf16[2,64,512]{2,1,0:T(8,128)(2,1)S(1)}, bf16[2,64,512]{2,1,0:T(8,128)(2,1)S(1)}, u32[]{:S(2)}, u32[]{:S(2)}) collective-permute-start(bf16[2,64,512]{2,1,0:T(8,128)(2,1)S(1)} %fusion.28), channel_id=1, source_target_pairs={{0,8},{1,9},{2,10},{3,11},{4,12},{5,13},{6,14},{7,15},{8,0},{9,1},... | collective-permute-start | bytes 393224 | tf_op jit(solution)/shard_map/ppermute | solution.py:91
  279.3 10.1 %collective-permute-start.19 = (bf16[64,512]{1,0:T(8,128)(2,1)S(1)}, bf16[64,512]{1,0:T(8,128)(2,1)S(1)}, u32[]{:S(2)}, u32[]{:S(2)}) collective-permute-start(bf16[64,512]{1,0:T(8,128)(2,1)S(1)} %fusion.40), channel_id=1, source_target_pairs={{0,4},{1,5},{2,6},{3,7},{4,0},{5,1},{6,2},{7,3},{8,12},{9,13},{10,... | collective-permute-start | bytes 196616 | tf_op jit(solution)/shard_map/ppermute | solution.py:91
  279.7 9.6 %collective-permute-start.14 = (bf16[64,512]{1,0:T(8,128)(2,1)S(1)}, bf16[64,512]{1,0:T(8,128)(2,1)S(1)}, u32[]{:S(2)}, u32[]{:S(2)}) collective-permute-start(bf16[64,512]{1,0:T(8,128)(2,1)S(1)} %fusion.39), channel_id=1, source_target_pairs={{0,4},{1,5},{2,6},{3,7},{4,0},{5,1},{6,2},{7,3},{8,12},{9,13},{10,... | collective-permute-start | bytes 196616 | tf_op jit(solution)/shard_map/ppermute | solution.py:91
  285.0 3.2 %collective-permute-start.5 = (bf16[64,512]{1,0:T(8,128)(2,1)S(1)}, bf16[64,512]{1,0:T(8,128)(2,1)S(1)}, u32[]{:S(2)}, u32[]{:S(2)}) collective-permute-start(bf16[64,512]{1,0:T(8,128)(2,1)S(1)} %fusion.37), channel_id=1, source_target_pairs={{0,4},{1,5},{2,6},{3,7},{4,0},{5,1},{6,2},{7,3},{8,12},{9,13},{10,... | collective-permute-start | bytes 196616 | tf_op jit(solution)/shard_map/ppermute | solution.py:91
  285.2 4.2 %collective-permute-start.9 = (bf16[64,512]{1,0:T(8,128)(2,1)S(1)}, bf16[64,512]{1,0:T(8,128)(2,1)S(1)}, u32[]{:S(2)}, u32[]{:S(2)}) collective-permute-start(bf16[64,512]{1,0:T(8,128)(2,1)S(1)} %fusion.38), channel_id=1, source_target_pairs={{0,4},{1,5},{2,6},{3,7},{4,0},{5,1},{6,2},{7,3},{8,12},{9,13},{10,... | collective-permute-start | bytes 196616 | tf_op jit(solution)/shard_map/ppermute | solution.py:91
  (4 other events, 19.3 us)
Sparse Core Ops, SparseCore 0:
  19.8 66.7 all-gather.1

commit v2 on v1

--- a/solution.py
+++ b/solution.py
@@ -14,6 +14,8 @@
 
 EPSILON = 1e-06
 PIECES = 2
+EARLY = 1
+GROUPED = True
 
 
 def rms_normed(hidden_in, norm_gain):
@@ -69,29 +71,56 @@
     return block.reshape(-1, width)
 
 
-def summed(partial):
-    count = lax.axis_size("expert")
-    index = lax.axis_index("expert")
+def stage_bits(count):
     if count & (count - 1):
-        return lax.psum_scatter(
-            partial.astype(jnp.bfloat16), "expert", scatter_dimension=0, tiled=True
-        )
+        return [None]
     total_bits = count.bit_length() - 1
     low_bits = min(2, total_bits)
-    order = list(range(low_bits)) + list(range(total_bits - 1, low_bits - 1, -1))
+    order = [(bit,) for bit in range(low_bits)]
+    high = list(range(total_bits - 1, low_bits - 1, -1))
+    while high:
+        order.append(tuple(high[:2]))
+        high = high[2:]
+    return order
+
+
+def staged(partial, count):
     rows, width = partial.shape
-    left = sorted(order)
-    kept = partial.reshape((2,) * total_bits + (rows // count, width))
-    for bit in order:
-        axis = len(left) - 1 - left.index(bit)
-        side = (index >> bit) & 1
-        out = lax.dynamic_index_in_dim(kept, 1 - side, axis, keepdims=False)
-        own = lax.dynamic_index_in_dim(kept, side, axis, keepdims=False)
-        pairs = [(i, i ^ (1 << bit)) for i in range(count)]
-        came = lax.ppermute(out.astype(jnp.bfloat16), "expert", pairs)
-        kept = own.astype(jnp.float32) + came.astype(jnp.float32)
-        left.remove(bit)
-    return kept.astype(jnp.bfloat16)
+    if count & (count - 1):
+        return partial
+    return partial.reshape((2,) * (count.bit_length() - 1) + (rows // count, width))
+
+
+def halved(kept, number):
+    count = lax.axis_size("expert")
+    order = stage_bits(count)
+    bits = order[number]
+    if bits is None:
+        return lax.psum_scatter(kept, "expert", scatter_dimension=0, tiled=True)
+    left = sorted(sum(order[number:], ()))
+    index = lax.axis_index("expert")
+
+    def picked(flips):
+        part = kept
+        remaining = list(left)
+        for bit in bits:
+            axis = len(remaining) - 1 - remaining.index(bit)
+            side = (index >> bit) & 1
+            side = 1 - side if bit in flips else side
+            part = lax.dynamic_index_in_dim(part, side, axis, keepdims=False)
+            remaining.remove(bit)
+        return part
+
+    choices = [()]
+    for bit in bits:
+        choices = choices + [flips + (bit,) for flips in choices]
+    total = picked(()).astype(jnp.float32)
+    for flips in choices[1:]:
+        mask = sum(1 << bit for bit in flips)
+        pairs = [(i, i ^ mask) for i in range(count)]
+        came = lax.ppermute(picked(flips).astype(jnp.bfloat16), "expert", pairs)
+        total = total + came.astype(jnp.float32)
+    return total
 
 
 def local(
@@ -161,17 +190,50 @@
             hidden_units, units, place * unit_width, axis=1
         )
 
+    def scaled(down_weight):
+        expert_out = jnp.dot(hidden_units, down_weight, preferred_element_type=jnp.float32)
+        return (weight * expert_out).astype(jnp.bfloat16)
+
     out_width = down_pieces[0].shape[1]
+    keys = [(step, number) for number in range(PIECES) for step in range(parts)]
+    weights = [
+        down_pieces[number] if step == 0 else shifted(down_pieces[number], step)
+        for step, number in keys
+    ]
+    device_count = lax.axis_size("expert")
+    stages = len(stage_bits(device_count))
+    if GROUPED:
+        grouped = [[0], list(range(1, len(keys) - 1)), [len(keys) - 1]]
+    else:
+        grouped = [[i] for i in range(len(keys))]
+    joined = [
+        weights[group[0]]
+        if len(group) == 1
+        else jnp.concatenate([weights[i] for i in group], axis=1)
+        for group in grouped
+    ]
+    chains = []
+    reach = min(EARLY, stages)
+    for number, weight_ in enumerate(joined):
+        if number and reach:
+            chains[-1], weight_ = lax.optimization_barrier((chains[-1], weight_))
+        if number:
+            for stage in range(reach, stages):
+                chains[-1] = halved(chains[-1], stage)
+        chain = staged(scaled(weight_), device_count)
+        for stage in range(reach):
+            chain = halved(chain, stage)
+        chains.append(chain)
+    for stage in range(reach, stages):
+        chains[-1] = halved(chains[-1], stage)
+    reduced = jnp.concatenate(chains, axis=1).astype(jnp.bfloat16)
     mixed_out = jnp.zeros((tok_count, width), jnp.bfloat16)
-    for step in range(parts):
-        for number, down_own in enumerate(down_pieces):
-            down_weight = down_own if step == 0 else shifted(down_own, step)
-            expert_out = jnp.dot(hidden_units, down_weight, preferred_element_type=jnp.float32)
-            reduced = summed((weight * expert_out).astype(jnp.bfloat16))
-            place = ((part + parts - step) % parts) * PIECES + number
-            mixed_out = lax.dynamic_update_slice_in_dim(
-                mixed_out, reduced, place * out_width, axis=1
-            )
+    for place_, (step, number) in enumerate(keys):
+        place = ((part + parts - step) % parts) * PIECES + number
+        block = lax.slice_in_dim(reduced, place_ * out_width, (place_ + 1) * out_width, axis=1)
+        mixed_out = lax.dynamic_update_slice_in_dim(
+            mixed_out, block, place * out_width, axis=1
+        )
     return (attended, mixed_out)
 
 

time: 301 us -> 286 us (0.950)
  the two profiles are of different devices: /device:TPU:13 before, /device:TPU:0 now
where the time goes in v2:
time: 286 us; the launch traced here: 285 us
  waiting for transfers between devices  159 us (56%)
  starting transfers between devices  54.3 us (19%)
  matrix products  27.9 us (10%)
  local copies, waits for them, and re-layouts  16.2 us (6%)
  between operations  14.5 us (5%)
  other arithmetic  12.9 us (5%)
    all_to_all x4, waiting for transfers between devices, moved(): lax.all_to_all(own, 'expert', split_axis=0, concat_axis=0, tiled=True)  98.9 us
    ppermute x4, waiting for transfers between devices, shifted(): lax.ppermute(value, 'groups', [(i, (i + step) % count) for i in range(cou...  37.9 us
    all_to_all x4, starting transfers between devices, moved(): lax.all_to_all(own, 'expert', split_axis=0, concat_axis=0, tiled=True)  31.1 us
    ppermute x15, waiting for transfers between devices, halved(): came = lax.ppermute(picked(flips).astype(jnp.bfloat16), 'expert', pairs)  22.4 us
    ppermute x15, starting transfers between devices, halved(): came = lax.ppermute(picked(flips).astype(jnp.bfloat16), 'expert', pairs)  17.7 us
    dot_general x2, matrix products, local(): jnp.dot(all_rows, gate_weight, preferred_element_type=jnp.float32)  8.87 us
    dot_general x2, matrix products, local(): up_proj = jnp.dot(all_rows, up_weight, preferred_element_type=jnp.float32)  7.92 us
    dynamic_slice x3, local copies, waits for them, and re-layouts, moved(): lax.dynamic_slice_in_dim(train, (part * pieces + piece) * width, width, a...  6.74 us
  transfers between devices with their start and end apart: 24, of which 12 were waited for; matrix products, arithmetic and copies ran while one was open for 15% of the time, Pallas kernels for 0%

profile of v2, /device:TPU:0, one launch (start us, length us, event | category | flops | bytes accessed | tf_op | source)
XLA Modules:
  0.0 284.9 jit_solution(2901623583065921570)
XLA Ops:
  13.2 2.6 constant_dynamic-slice_fusion.4
  15.8 7.5 %all-to-all-start.2 = ((bf16[16,48,512]{2,1,0:T(8,128)(2,1)}), bf16[16,48,512]{2,1,0:T(8,128)(2,1)}, u32[]{:S(2)}, u32[]{:S(2)}) async-start(bf16[16,48,512]{2,1,0:T(8,128)(2,1)} %get-tuple-element.11), calls=%async_computation.2 | async-start | bytes 1572864 | tf_op jit(solution)/shard_map/all_to_all | solution.py:70
  24.6 26.3 %all-to-all-done.2 = bf16[16,48,512]{2,1,0:T(8,128)(2,1)} async-done(((bf16[16,48,512]{2,1,0:T(8,128)(2,1)}), bf16[16,48,512]{2,1,0:T(8,128)(2,1)}, u32[]{:S(2)}, u32[]{:S(2)}) %all-to-all-start.2) | async-done | bytes 786464 | tf_op jit(solution)/shard_map/all_to_all | solution.py:70
  50.9 5.5 %all-to-all-start = ((bf16[16,128,384]{2,1,0:T(8,128)(2,1)}), bf16[16,128,384]{2,1,0:T(8,128)(2,1)}, u32[]{:S(2)}, u32[]{:S(2)}) async-start(bf16[16,128,384]{2,1,0:T(8,128)(2,1)} %constant_dynamic-slice_fusion.9), calls=%async_computation | async-start | bytes 3145728 | tf_op jit(solution)/shard_map/all_to_all | solution.py:70
  56.5 2.8 constant_dynamic-slice_fusion.8
  59.2 44.4 %all-to-all-done = bf16[16,128,384]{2,1,0:T(8,128)(2,1)} async-done(((bf16[16,128,384]{2,1,0:T(8,128)(2,1)}), bf16[16,128,384]{2,1,0:T(8,128)(2,1)}, u32[]{:S(2)}, u32[]{:S(2)}) %all-to-all-start) | async-done | bytes 1572896 | tf_op jit(solution)/shard_map/all_to_all | solution.py:70
  103.6 9.0 %all-to-all-start.1 = ((bf16[16,128,384]{2,1,0:T(8,128)(2,1)}), bf16[16,128,384]{2,1,0:T(8,128)(2,1)}, u32[]{:S(2)}, u32[]{:S(2)}) async-start(bf16[16,128,384]{2,1,0:T(8,128)(2,1)} %constant_dynamic-slice_fusion.8), calls=%async_computation.1 | async-start | bytes 3145728 | tf_op jit(solution)/shard_map/all_to_all | solution.py:70
  112.6 1.7 collective-permute-start
  116.3 28.2 %all-to-all-done.1 = bf16[16,128,384]{2,1,0:T(8,128)(2,1)} async-done(((bf16[16,128,384]{2,1,0:T(8,128)(2,1)}), bf16[16,128,384]{2,1,0:T(8,128)(2,1)}, u32[]{:S(2)}, u32[]{:S(2)}) %all-to-all-start.1) | async-done | bytes 1572896 | tf_op jit(solution)/shard_map/all_to_all | solution.py:70
  144.5 9.2 %all-to-all-start.3 = ((bf16[16,48,512]{2,1,0:T(8,128)(2,1)}), bf16[16,48,512]{2,1,0:T(8,128)(2,1)}, u32[]{:S(2)}, u32[]{:S(2)}) async-start(bf16[16,48,512]{2,1,0:T(8,128)(2,1)} %get-tuple-element.10), calls=%async_computation.3 | async-start | bytes 1572864 | tf_op jit(solution)/shard_map/all_to_all | solution.py:70
  153.7 1.7 collective-permute-start.1
  155.4 5.1 %fusion.6 = f32[1024,384]{1,0:T(8,128)S(1)} fusion(bf16[2048,384]{1,0:T(8,128)(2,1)} %bitcast.6, bf16[1024,2176]{1,0:T(8,128)(2,1)} %all-gather.2.cloned.1.call-done), kind=kOutput, calls=%fused_computation.7 | convolution fusion | flops 1610612736 | bytes 7340032 | tf_op jit(solution)/shard_map/dot_general | solution.py:185
  160.5 3.7 %fusion.2 = f32[1024,384]{1,0:T(8,128)S(1)} fusion(bf16[2048,384]{1,0:T(8,128)(2,1)} %collective-permute-done, bf16[1024,2176]{1,0:T(8,128)(2,1)S(1)} %copy-done.8), kind=kOutput, calls=%fused_computation.3 | convolution fusion | flops 1610612736 | bytes 7340032 | tf_op jit(solution)/shard_map/dot_general | solution.py:185
  164.4 4.0 %fusion.10 = bf16[1024,768]{1,0:T(8,128)(2,1)S(1)} fusion(bf16[1024,768]{1,0:T(8,128)(2,1)S(1)} %broadcast_in_dim.63, s32[]{:T(128)S(6)} %select_n.140, bf16[2048,384]{1,0:T(8,128)(2,1)} %bitcast.7, bf16[1024,2176]{1,0:T(8,128)(2,1)S(1)} %copy-done.8, f32[1024,384]{1,0:T(8,128)S(1)} %fusion.6), kind=kOutput, calls=%fused_computation.15 | convolution fusion | flops 1612972032 | bytes 8126468 | tf_op jit(solution)/shard_map/dot_general | solution.py:186
  168.3 31.8 %collective-permute-done.1 = bf16[2048,384]{1,0:T(8,128)(2,1)} collective-permute-done((bf16[2048,384]{1,0:T(8,128)(2,1)}, bf16[2048,384]{1,0:T(8,128)(2,1)}, u32[]{:S(2)}, u32[]{:S(2)}) %collective-permute-start.1) | collective-permute-done | bytes 1572896 | tf_op jit(solution)/shard_map/ppermute | solution.py:64
  200.1 4.0 %fusion.16 = bf16[1024,768]{1,0:T(8,128)(2,1)S(1)} fusion(bf16[1024,768]{1,0:T(8,128)(2,1)S(1)} %fusion.10, s32[]{:T(128)S(6)} %select_n.142, f32[1024,384]{1,0:T(8,128)S(1)} %fusion.2, bf16[2048,384]{1,0:T(8,128)(2,1)} %collective-permute-done.1, bf16[1024,2176]{1,0:T(8,128)(2,1)S(1)} %copy-done.8), kind=kOutput, calls=%fused_computation.27 | convolution fusion | flops 1612972032 | bytes 8126468 | tf_op jit(solution)/shard_map/dot_general | solution.py:186
  204.3 2.5 multiply_convert_fusion.2
  209.0 1.6 pad_maximum_fusion
  210.8 2.3 convert_add_fusion.2
  213.1 1.8 multiply_convert_fusion
  218.1 1.8 fusion.25
  219.9 1.6 collective-permute-start.4
  223.8 2.0 fusion.15
  229.6 2.6 collective-permute-start.5
  234.1 1.7 convert_add_fusion
  235.8 6.0 %collective-permute-done.9 = bf16[768,512]{1,0:T(8,128)(2,1)} collective-permute-done((bf16[768,512]{1,0:T(8,128)(2,1)}, bf16[768,512]{1,0:T(8,128)(2,1)}, u32[]{:S(2)}, u32[]{:S(2)}) %collective-permute-start.9) | collective-permute-done | bytes 786464 | tf_op jit(solution)/shard_map/ppermute | solution.py:64
  242.4 2.1 multiply_convert_fusion.1
  244.8 10.0 %collective-permute-done.10 = bf16[2,2,64,1024]{3,2,1,0:T(8,128)(2,1)S(1)} collective-permute-done((bf16[2,2,64,1024]{3,2,1,0:T(8,128)(2,1)S(1)}, bf16[2,2,64,1024]{3,2,1,0:T(8,128)(2,1)S(1)}, u32[]{:S(2)}, u32[]{:S(2)}) %collective-permute-start.10) | collective-permute-done | bytes 524320 | tf_op jit(solution)/shard_map/ppermute | solution.py:121
  255.1 2.4 collective-permute-start.11
  260.2 6.4 %collective-permute-done.11 = bf16[64,1024]{1,0:T(8,128)(2,1)S(1)} collective-permute-done((bf16[64,1024]{1,0:T(8,128)(2,1)S(1)}, bf16[64,1024]{1,0:T(8,128)(2,1)S(1)}, u32[]{:S(2)}, u32[]{:S(2)}) %collective-permute-start.11) | collective-permute-done | bytes 131104 | tf_op jit(solution)/shard_map/ppermute | solution.py:121
  266.9 4.3 %collective-permute-start.16 = (bf16[64,512]{1,0:T(8,128)(2,1)S(1)}, bf16[64,512]{1,0:T(8,128)(2,1)S(1)}, u32[]{:S(2)}, u32[]{:S(2)}) collective-permute-start(bf16[64,512]{1,0:T(8,128)(2,1)S(1)} %get-tuple-element.21), channel_id=1, source_target_pairs={{0,8},{1,9},{2,10},{3,11},{4,12},{5,13},{6,14},{7,15},{8,0},{9,1},... | collective-permute-start | bytes 196616 | tf_op jit(solution)/shard_map/ppermute | solution.py:121
  272.7 2.6 collective-permute-done.16
  (103 shorter events, 31.3 us)
Async XLA Ops:
  7.2 16.1 %copy-start = (bf16[16,128,768]{2,1,0:T(8,128)(2,1)S(1)}, bf16[16,128,768]{2,1,0:T(8,128)(2,1)}, u32[]{:S(2)}) copy-start(bf16[16,128,768]{2,1,0:T(8,128)(2,1)} %param.23) | copy-start | bytes 9437188
  7.2 148.2 %all-gather.2.cloned.1.call-start = ((), (), s32[]{:S(2)}) async-start(), calls=%async_computation.4 | async-start | bytes 4734976 | tf_op jit(solution)/shard_map/all_gather | solution.py:166
  15.8 35.1 %all-to-all-start.2 = ((bf16[16,48,512]{2,1,0:T(8,128)(2,1)}), bf16[16,48,512]{2,1,0:T(8,128)(2,1)}, u32[]{:S(2)}, u32[]{:S(2)}) async-start(bf16[16,48,512]{2,1,0:T(8,128)(2,1)} %get-tuple-element.11), calls=%async_computation.2 | async-start | bytes 1572864 | tf_op jit(solution)/shard_map/all_to_all | solution.py:70
  50.9 52.7 %all-to-all-start = ((bf16[16,128,384]{2,1,0:T(8,128)(2,1)}), bf16[16,128,384]{2,1,0:T(8,128)(2,1)}, u32[]{:S(2)}, u32[]{:S(2)}) async-start(bf16[16,128,384]{2,1,0:T(8,128)(2,1)} %constant_dynamic-slice_fusion.9), calls=%async_computation | async-start | bytes 3145728 | tf_op jit(solution)/shard_map/all_to_all | solution.py:70
  59.2 55.1 %copy-start.12 = (s32[8]{0:T(128)S(1)}, s32[8]{0:T(128)}, u32[]{:S(2)}) copy-start(s32[8]{0:T(128)} %param.18) | copy-start | bytes 100
  59.2 55.1 %copy-start.7 = (bf16[8,4096]{1,0:T(8,128)(2,1)S(1)}, bf16[8,4096]{1,0:T(8,128)(2,1)}, u32[]{:S(2)}) copy-start(bf16[8,4096]{1,0:T(8,128)(2,1)} %param.13) | copy-start | bytes 196612
  103.6 40.9 %all-to-all-start.1 = ((bf16[16,128,384]{2,1,0:T(8,128)(2,1)}), bf16[16,128,384]{2,1,0:T(8,128)(2,1)}, u32[]{:S(2)}, u32[]{:S(2)}) async-start(bf16[16,128,384]{2,1,0:T(8,128)(2,1)} %constant_dynamic-slice_fusion.8), calls=%async_computation.1 | async-start | bytes 3145728 | tf_op jit(solution)/shard_map/all_to_all | solution.py:70
  112.6 47.9 %collective-permute-start = (bf16[2048,384]{1,0:T(8,128)(2,1)}, bf16[2048,384]{1,0:T(8,128)(2,1)}, u32[]{:S(2)}, u32[]{:S(2)}) collective-permute-start(bf16[2048,384]{1,0:T(8,128)(2,1)} %bitcast.6), channel_id=1, source_target_pairs={{0,16},{16,0},{1,17},{17,1},{2,18},{18,2},{3,19},{19,3},{4,20},{20... | collective-permute-start | bytes 4718600 | tf_op jit(solution)/shard_map/ppermute | solution.py:64
  115.9 93.1 %collective-permute-start.3 = (bf16[768,512]{1,0:T(8,128)(2,1)}, bf16[768,512]{1,0:T(8,128)(2,1)}, u32[]{:S(2)}, u32[]{:S(2)}) collective-permute-start(bf16[768,512]{1,0:T(8,128)(2,1)} %bitcast.8), channel_id=1, source_target_pairs={{0,16},{16,0},{1,17},{17,1},{2,18},{18,2},{3,19},{19,3},{4,20},{20... | collective-permute-start | bytes 2359304 | tf_op jit(solution)/shard_map/ppermute | solution.py:64
  144.5 64.4 %all-to-all-start.3 = ((bf16[16,48,512]{2,1,0:T(8,128)(2,1)}), bf16[16,48,512]{2,1,0:T(8,128)(2,1)}, u32[]{:S(2)}, u32[]{:S(2)}) async-start(bf16[16,48,512]{2,1,0:T(8,128)(2,1)} %get-tuple-element.10), calls=%async_computation.3 | async-start | bytes 1572864 | tf_op jit(solution)/shard_map/all_to_all | solution.py:70
  153.7 46.5 %collective-permute-start.1 = (bf16[2048,384]{1,0:T(8,128)(2,1)}, bf16[2048,384]{1,0:T(8,128)(2,1)}, u32[]{:S(2)}, u32[]{:S(2)}) collective-permute-start(bf16[2048,384]{1,0:T(8,128)(2,1)} %bitcast.7), channel_id=1, source_target_pairs={{0,16},{16,0},{1,17},{17,1},{2,18},{18,2},{3,19},{19,3},{4,20},{20... | collective-permute-start | bytes 4718600 | tf_op jit(solution)/shard_map/ppermute | solution.py:64
  155.3 5.2 %copy-start.8 = (bf16[1024,2176]{1,0:T(8,128)(2,1)S(1)}, bf16[1024,2176]{1,0:T(8,128)(2,1)}, u32[]{:S(2)}) copy-start(bf16[1024,2176]{1,0:T(8,128)(2,1)} %all-gather.2.cloned.1.call-done) | copy-start | bytes 13369348
  204.3 8.8 %copy-start.9 = (f32[1024]{0:T(1024)}, f32[1024]{0:T(1024)S(1)}, u32[]{:S(2)}) copy-start(f32[1024]{0:T(1024)S(1)} %select_reduce_fusion) | copy-start | bytes 12292
  208.5 2.3 collective-permute-start.2
  217.1 17.0 %collective-permute-start.8 = (bf16[2,2,2,64,1024]{4,3,1,0,2:T(8,128)(2,1)}, bf16[2,2,2,64,1024]{4,3,1,0,2:T(8,128)(2,1)}, u32[]{:S(2)}, u32[]{:S(2)}) collective-permute-start(bf16[2,2,2,64,1024]{4,3,1,0,2:T(8,128)(2,1)} %bitcast.128), channel_id=1, source_target_pairs={{0,1},{1,0},{2,3},{3,2},{4,5},{5,4},{6,7},{7,6},{8,9},{9,8},{10,11... | collective-permute-start | bytes 3145736 | tf_op jit(solution)/shard_map/ppermute | solution.py:121
  219.9 8.6 %collective-permute-start.4 = (bf16[2,2,64,512]{3,2,1,0:T(8,128)(2,1)}, bf16[2,2,64,512]{3,2,1,0:T(8,128)(2,1)S(1)}, u32[]{:S(2)}, u32[]{:S(2)}) collective-permute-start(bf16[2,2,64,512]{3,2,1,0:T(8,128)(2,1)} %fusion.25), channel_id=1, source_target_pairs={{0,2},{1,3},{2,0},{3,1},{4,6},{5,7},{6,4},{7,5},{8,10},{9,11},{10,... | collective-permute-start | bytes 786440 | tf_op jit(solution)/shard_map/ppermute | solution.py:121
  222.2 19.6 %collective-permute-start.9 = (bf16[768,512]{1,0:T(8,128)(2,1)}, bf16[768,512]{1,0:T(8,128)(2,1)}, u32[]{:S(2)}, u32[]{:S(2)}) collective-permute-start(bf16[768,512]{1,0:T(8,128)(2,1)} %bitcast.12), channel_id=1, source_target_pairs={{0,16},{16,0},{1,17},{17,1},{2,18},{18,2},{3,19},{19,3},{4,20},{20... | collective-permute-start | bytes 2359304 | tf_op jit(solution)/shard_map/ppermute | solution.py:64
  227.3 6.8 %copy-start.1 = (bf16[2,2,2,1,64,1024]{5,4,3,2,1,0:T(8,128)(2,1)S(1)}, bf16[2,2,2,1,64,1024]{5,4,3,2,1,0:T(8,128)(2,1)}, u32[]{:S(2)}) copy-start(bf16[2,2,2,1,64,1024]{5,4,3,2,1,0:T(8,128)(2,1)} %get-tuple-element.12) | copy-start | bytes 3145732
  229.6 15.1 %collective-permute-start.5 = (bf16[64,512]{1,0:T(8,128)(2,1)S(1)}, bf16[64,512]{1,0:T(8,128)(2,1)S(1)}, u32[]{:S(2)}, u32[]{:S(2)}) collective-permute-start(bf16[64,512]{1,0:T(8,128)(2,1)S(1)} %get-tuple-element.24), channel_id=1, source_target_pairs={{0,8},{1,9},{2,10},{3,11},{4,12},{5,13},{6,14},{7,15},{8,0},{9,1},... | collective-permute-start | bytes 196616 | tf_op jit(solution)/shard_map/ppermute | solution.py:121
  232.2 12.5 %collective-permute-start.6 = (bf16[64,512]{1,0:T(8,128)(2,1)S(1)}, bf16[64,512]{1,0:T(8,128)(2,1)S(1)}, u32[]{:S(2)}, u32[]{:S(2)}) collective-permute-start(bf16[64,512]{1,0:T(8,128)(2,1)S(1)} %get-tuple-element.26), channel_id=1, source_target_pairs={{0,4},{1,5},{2,6},{3,7},{4,0},{5,1},{6,2},{7,3},{8,12},{9,13},{10,... | collective-permute-start | bytes 196616 | tf_op jit(solution)/shard_map/ppermute | solution.py:121
  233.7 11.0 %collective-permute-start.7 = (bf16[64,512]{1,0:T(8,128)(2,1)S(1)}, bf16[64,512]{1,0:T(8,128)(2,1)S(1)}, u32[]{:S(2)}, u32[]{:S(2)}) collective-permute-start(bf16[64,512]{1,0:T(8,128)(2,1)S(1)} %get-tuple-element.25), channel_id=1, source_target_pairs={{0,12},{1,13},{2,14},{3,15},{4,8},{5,9},{6,10},{7,11},{8,4},{9,5},... | collective-permute-start | bytes 196616 | tf_op jit(solution)/shard_map/ppermute | solution.py:121
  234.1 8.3 %copy-start.5 = (bf16[1024,768]{1,0:T(8,128)(2,1)S(1)}, bf16[1024,768]{1,0:T(8,128)(2,1)}, u32[]{:S(2)}) copy-start(bf16[1024,768]{1,0:T(8,128)(2,1)} %copy-done.3) | copy-start | bytes 4718596
  234.1 8.3 %copy-start.10 = (f32[1024]{0:T(1024)S(1)}, f32[1024]{0:T(1024)}, u32[]{:S(2)}) copy-start(f32[1024]{0:T(1024)} %copy-done.9) | copy-start | bytes 12292
  241.9 12.9 %collective-permute-start.10 = (bf16[2,2,64,1024]{3,2,1,0:T(8,128)(2,1)S(1)}, bf16[2,2,64,1024]{3,2,1,0:T(8,128)(2,1)S(1)}, u32[]{:S(2)}, u32[]{:S(2)}) collective-permute-start(bf16[2,2,64,1024]{3,2,1,0:T(8,128)(2,1)S(1)} %fusion.20), channel_id=1, source_target_pairs={{0,2},{1,3},{2,0},{3,1},{4,6},{5,7},{6,4},{7,5},{8,10},{9,11},{10,... | collective-permute-start | bytes 1572872 | tf_op jit(solution)/shard_map/ppermute | solution.py:121
  244.6 14.9 %collective-permute-start.14 = (bf16[2,2,2,64,512]{4,3,1,0,2:T(8,128)(2,1)S(1)}, bf16[2,2,2,64,512]{4,3,1,0,2:T(8,128)(2,1)S(1)}, u32[]{:S(2)}, u32[]{:S(2)}) collective-permute-start(bf16[2,2,2,64,512]{4,3,1,0,2:T(8,128)(2,1)S(1)} %bitcast.135), channel_id=1, source_target_pairs={{0,1},{1,0},{2,3},{3,2},{4,5},{5,4},{6,7},{7,6},{8,9},{9,8},{10,11... | collective-permute-start | bytes 1572872 | tf_op jit(solution)/shard_map/ppermute | solution.py:121
  255.1 11.5 %collective-permute-start.11 = (bf16[64,1024]{1,0:T(8,128)(2,1)S(1)}, bf16[64,1024]{1,0:T(8,128)(2,1)S(1)}, u32[]{:S(2)}, u32[]{:S(2)}) collective-permute-start(bf16[64,1024]{1,0:T(8,128)(2,1)S(1)} %get-tuple-element.16), channel_id=1, source_target_pairs={{0,8},{1,9},{2,10},{3,11},{4,12},{5,13},{6,14},{7,15},{8,0},{9,1},... | collective-permute-start | bytes 393224 | tf_op jit(solution)/shard_map/ppermute | solution.py:121
  257.5 9.1 %collective-permute-start.12 = (bf16[64,1024]{1,0:T(8,128)(2,1)S(1)}, bf16[64,1024]{1,0:T(8,128)(2,1)S(1)}, u32[]{:S(2)}, u32[]{:S(2)}) collective-permute-start(bf16[64,1024]{1,0:T(8,128)(2,1)S(1)} %get-tuple-element.18), channel_id=1, source_target_pairs={{0,4},{1,5},{2,6},{3,7},{4,0},{5,1},{6,2},{7,3},{8,12},{9,13},{10,... | collective-permute-start | bytes 393224 | tf_op jit(solution)/shard_map/ppermute | solution.py:121
  259.0 7.7 %collective-permute-start.13 = (bf16[64,1024]{1,0:T(8,128)(2,1)S(1)}, bf16[64,1024]{1,0:T(8,128)(2,1)S(1)}, u32[]{:S(2)}, u32[]{:S(2)}) collective-permute-start(bf16[64,1024]{1,0:T(8,128)(2,1)S(1)} %get-tuple-element.17), channel_id=1, source_target_pairs={{0,12},{1,13},{2,14},{3,15},{4,8},{5,9},{6,10},{7,11},{8,4},{9,5},... | collective-permute-start | bytes 393224 | tf_op jit(solution)/shard_map/ppermute | solution.py:121
  259.8 7.0 %collective-permute-start.15 = (bf16[2,2,64,512]{3,2,1,0:T(8,128)(2,1)S(1)}, bf16[2,2,64,512]{3,2,1,0:T(8,128)(2,1)S(1)}, u32[]{:S(2)}, u32[]{:S(2)}) collective-permute-start(bf16[2,2,64,512]{3,2,1,0:T(8,128)(2,1)S(1)} %fusion.26), channel_id=1, source_target_pairs={{0,2},{1,3},{2,0},{3,1},{4,6},{5,7},{6,4},{7,5},{8,10},{9,11},{10,... | collective-permute-start | bytes 786440 | tf_op jit(solution)/shard_map/ppermute | solution.py:121
  266.9 8.5 %collective-permute-start.16 = (bf16[64,512]{1,0:T(8,128)(2,1)S(1)}, bf16[64,512]{1,0:T(8,128)(2,1)S(1)}, u32[]{:S(2)}, u32[]{:S(2)}) collective-permute-start(bf16[64,512]{1,0:T(8,128)(2,1)S(1)} %get-tuple-element.21), channel_id=1, source_target_pairs={{0,8},{1,9},{2,10},{3,11},{4,12},{5,13},{6,14},{7,15},{8,0},{9,1},... | collective-permute-start | bytes 196616 | tf_op jit(solution)/shard_map/ppermute | solution.py:121
  271.2 4.6 %collective-permute-start.17 = (bf16[64,512]{1,0:T(8,128)(2,1)S(1)}, bf16[64,512]{1,0:T(8,128)(2,1)S(1)}, u32[]{:S(2)}, u32[]{:S(2)}) collective-permute-start(bf16[64,512]{1,0:T(8,128)(2,1)S(1)} %get-tuple-element.23), channel_id=1, source_target_pairs={{0,4},{1,5},{2,6},{3,7},{4,0},{5,1},{6,2},{7,3},{8,12},{9,13},{10,... | collective-permute-start | bytes 196616 | tf_op jit(solution)/shard_map/ppermute | solution.py:121
  271.2 6.2 %collective-permute-start.18 = (bf16[64,512]{1,0:T(8,128)(2,1)S(1)}, bf16[64,512]{1,0:T(8,128)(2,1)S(1)}, u32[]{:S(2)}, u32[]{:S(2)}) collective-permute-start(bf16[64,512]{1,0:T(8,128)(2,1)S(1)} %get-tuple-element.22), channel_id=1, source_target_pairs={{0,12},{1,13},{2,14},{3,15},{4,8},{5,9},{6,10},{7,11},{8,4},{9,5},... | collective-permute-start | bytes 196616 | tf_op jit(solution)/shard_map/ppermute | solution.py:121
  (5 other events, 9.5 us)
Sparse Core Ops, SparseCore 0:
  13.3 87.8 all-gather.1
